TPU v7x, 32 devices: a 4x2x2 block of a 4x4x8 slice. The times are simulated.
32 devices in a mesh: dp: 4 (over y, z), sp: 8 (over x, core).
Axes of the slice: x: 4, y: 2, z: 2, core: 2. Of those that a mesh axis runs over, the one named last changes fastest.
The devices are a block of a 4x4x8 slice.
Arguments:
- hidden: bfloat16 [8192, 2048], P(('dp', 'sp')), parts along dimension 0
- seg_ids: int32 [8192], P(('dp', 'sp')), parts along dimension 0
- norm_kv: bfloat16 [2048], replicated
- w_key: bfloat16 [2048, 32, 64], replicated
- w_value: bfloat16 [2048, 32, 64], replicated
- norm_attn: bfloat16 [1, 2048], replicated
- w_query: bfloat16 [1, 2048, 32, 64], replicated
- w_out: bfloat16 [1, 32, 64, 2048], replicated
- norm_mlp: bfloat16 [1, 2048], replicated
- w_gate: bfloat16 [1, 2048, 8192], replicated
- w_up: bfloat16 [1, 2048, 8192], replicated
- w_down: bfloat16 [1, 8192, 2048], replicated
Outputs:
- output: bfloat16 [8192, 2048], P(('dp', 'sp')), parts along dimension 0
There are 4 independent parts. A program takes and returns all parts, laid end to end along the dimension named above; an argument that names none is the same for every part.
All inputs are finite; a program needn't handle non-finite values.
Results may differ from a plain program's by a relative error of at most 0.0131936.
Values are sent between devices in bfloat16 or wider.
A program may use at most 768 MiB of HBM per device.

v0:
```python
import jax
import jax.numpy as jnp
from jax import lax
from jax.sharding import PartitionSpec as P

NORM_EPS = 1e-6


def rms_norm(values, gain):
    val32 = values.astype(jnp.float32)
    inv_rms = lax.rsqrt(jnp.mean(val32 * val32, axis=-1, keepdims=True) + NORM_EPS)
    return (val32 * inv_rms * gain.astype(jnp.float32)).astype(jnp.bfloat16)


def cross_layer(state, key_all, val_all, allowed, g_attn, query_w, out_w, g_mlp, gate_w, up_w, down_w):
    d_model, q_heads, head_dim = query_w.shape
    kv_heads = key_all.shape[1]
    q_per_kv = q_heads // kv_heads
    u_attn = rms_norm(state, g_attn)
    query = jnp.einsum('td,drgk->trgk', u_attn, query_w.reshape(d_model, q_per_kv, kv_heads, head_dim), preferred_element_type=jnp.float32).astype(jnp.bfloat16)
    scores = jnp.einsum('qrgd,kgd->grqk', query, key_all, preferred_element_type=jnp.float32) * (head_dim ** -0.5)
    scores = jnp.where(allowed[None, None], scores, -1e30)
    probs = jax.nn.softmax(scores, axis=-1).astype(jnp.bfloat16)
    mixed = jnp.einsum('grqk,kgd->qrgd', probs, val_all, preferred_element_type=jnp.float32).astype(jnp.bfloat16)
    attn_out = jnp.einsum('qrgd,rgdm->qm', mixed, out_w.reshape(q_per_kv, kv_heads, head_dim, d_model), preferred_element_type=jnp.float32).astype(jnp.bfloat16)
    state = state + attn_out
    u_mlp = rms_norm(state, g_mlp)
    gate_val = jnp.dot(u_mlp, gate_w, preferred_element_type=jnp.float32).astype(jnp.bfloat16)
    up_val = jnp.dot(u_mlp, up_w, preferred_element_type=jnp.float32).astype(jnp.bfloat16)
    act_val = (jax.nn.silu(gate_val.astype(jnp.float32)) * up_val.astype(jnp.float32)).astype(jnp.bfloat16)
    down_val = jnp.dot(act_val, down_w, preferred_element_type=jnp.float32).astype(jnp.bfloat16)
    return state + down_val


def solution(mesh):
    def body(hidden, seg_ids, norm_kv, w_key, w_value, norm_attn, w_query, w_out, norm_mlp, w_gate, w_up, w_down):
        tokens = hidden.shape[0]
        layers = w_query.shape[0]
        shard = lax.axis_index('sp')
        u_kv = rms_norm(hidden, norm_kv)
        key_loc = jnp.einsum('td,dgk->tgk', u_kv, w_key, preferred_element_type=jnp.float32).astype(jnp.bfloat16)
        val_loc = jnp.einsum('td,dgk->tgk', u_kv, w_value, preferred_element_type=jnp.float32).astype(jnp.bfloat16)
        key_all = lax.all_gather(key_loc, 'sp', axis=0, tiled=True)
        val_all = lax.all_gather(val_loc, 'sp', axis=0, tiled=True)
        seg_all = lax.all_gather(seg_ids, 'sp', axis=0, tiled=True)
        seq_len = key_all.shape[0]
        q_pos = shard * tokens + jnp.arange(tokens, dtype=jnp.int32)
        k_pos = jnp.arange(seq_len, dtype=jnp.int32)
        allowed = (k_pos[None, :] <= q_pos[:, None]) & (seg_all[None, :] == seg_ids[:, None])
        state = hidden
        for layer in range(layers):
            state = cross_layer(state, key_all, val_all, allowed, norm_attn[layer], w_query[layer], w_out[layer], norm_mlp[layer], w_gate[layer], w_up[layer], w_down[layer])
        return state

    row_spec = P(('dp', 'sp'), None)
    in_specs = (row_spec, P(('dp', 'sp'))) + (P(),) * 10
    return jax.shard_map(body, mesh=mesh, in_specs=in_specs, out_specs=row_spec, check_vma=False)
```

profile of v0, /device:TPU:81, one launch (start us, length us, event | category | flops | bytes accessed | tf_op | source)
XLA Modules:
  0.0 208.3 jit_solution(13465408847830965764)
XLA Ops:
  6.5 0.0 all-gather.6.cloned.1.call-start
  6.6 1.5 fusion.56
  8.1 0.7 convert_element_type.67
  8.8 0.0 copy-start
  8.8 6.4 %fusion.82 = f32[256,2048]{0,1:S(1)} fusion(bf16[2048,2048]{0,1:T(8,128)(2,1)} %bitcast.102, bf16[256,2048]{1,0:T(8,128)(2,1)} %param.12, f32[2048]{0:T(1024)S(1)} %convert_element_type.67, f32[256]{0:T(256)S(1)} %add_rsqrt_fusion.1), kind=kOutput, calls=%fused_computation.56 | convolution fusion | flops 2149580800 | bytes 11543552
  15.2 1.1 convert_element_type.70
  16.3 0.1 all-gather.6.cloned.1.call-update
  16.4 0.1 all-gather.4.cloned.1.call-start
  16.5 0.0 copy-done
  16.5 0.0 copy-start.1
  16.5 0.0 copy-start.2
  16.5 0.0 copy-start.3
  16.5 6.0 %fusion.84 = f32[256,2048]{0,1:S(1)} fusion(bf16[2048,2048]{0,1:T(8,128)(2,1)} %bitcast.103, bf16[256,2048]{1,0:T(8,128)(2,1)S(1)} %copy-done, f32[2048]{0:T(1024)S(1)} %convert_element_type.67, f32[256]{0:T(256)S(1)} %add_rsqrt_fusion.1), kind=kOutput, calls=%fused_computation.57 | convolution fusion | flops 2149580800 | bytes 11543552
  22.5 1.1 convert_element_type.69
  23.6 0.1 all-gather.4.cloned.1.call-update
  23.7 0.0 copy-done.1
  23.7 0.0 copy-done.2
  23.8 0.0 copy-done.3
  23.8 12.5 %all-gather = s32[8,1,256]{2,1,0:T(1,128)S(1)} all-gather(s32[1,1,256]{2,1,0:T(1,128)S(1)} %bitcast.101), channel_id=1, replica_groups=mesh['dp'=4,'sp'=8] {'sp'}, dimensions={0}, use_global_device_ids=true | all-gather | bytes 9216 | tf_op jit(solution)/shard_map/all_gather | solution.py:45
  36.3 0.6 fusion.60
  36.9 7.2 %fusion.70 = f32[256,2048]{0,1} fusion(bf16[2048,2048]{0,1:T(8,128)(2,1)} %bitcast.104, bf16[256,2048]{1,0:T(8,128)(2,1)S(1)} %copy-done, f32[2048]{0:T(1024)S(1)} %bitcast.100, f32[256]{0:T(256)S(1)} %add_rsqrt_fusion.1), kind=kOutput, calls=%fused_computation.47 | convolution fusion | flops 2149580800 | bytes 11543552
  44.1 26.8 %all-gather.6.cloned.1.call-done = bf16[2048,32,64]{0,2,1:T(8,128)(2,1)} async-done(((bf16[256,32,64]{0,2,1:T(8,128)(2,1)}), bf16[2048,32,64]{0,2,1:T(8,128)(2,1)}) %all-gather.6.cloned.1.call-update) | async-done | bytes 8388624 | tf_op jit(solution)/shard_map/all_gather | solution.py:43
  70.9 27.2 %fusion.1 = (f32[32,256]{1,0:T(8,128)S(1)}, f32[32,2048,256]{2,1,0:T(8,128)}) fusion(pred[256,2048]{0,1:T(8,128)(4,1)S(1)} %fusion.60, bf16[2048,32,64]{0,2,1:T(8,128)(2,1)} %all-gather.6.cloned.1.call-done, f32[256,32,64]{0,2,1:T(8,128)} %bitcast.94), kind=kOutput, calls=%fused_computation.4 | convolution fusion | flops 2198331392 | bytes 78151680 | tf_op jit(solution)/shard_map/qrgd,kgd->grqk/dot_general | solution.py:21
  98.1 21.6 %fusion = f32[32,256]{1,0:T(8,128)S(1)} fusion(f32[32,2048,256]{2,1,0:T(8,128)} %get-tuple-element.6, f32[32,256]{1,0:T(8,128)S(1)} %get-tuple-element.5, pred[256,2048]{0,1:T(8,128)(4,1)S(1)} %fusion.60), kind=kLoop, calls=%fused_computation.3 | loop fusion | flops 67100672 | bytes 67698688 | tf_op jit(solution)/shard_map/reduce_sum | solution.py:23
  119.7 3.6 %all-gather.4.cloned.1.call-done = bf16[2048,32,64]{0,2,1:T(8,128)(2,1)} async-done(((bf16[256,32,64]{0,2,1:T(8,128)(2,1)}), bf16[2048,32,64]{0,2,1:T(8,128)(2,1)}) %all-gather.4.cloned.1.call-update) | async-done | bytes 8388624 | tf_op jit(solution)/shard_map/all_gather | solution.py:44
  123.3 27.6 %fusion.64 = bf16[256,32,64]{0,2,1:T(8,128)(2,1)S(1)} fusion(bf16[2048,32,64]{0,2,1:T(8,128)(2,1)} %all-gather.4.cloned.1.call-done, f32[32,256]{1,0:T(8,128)S(1)} %fusion, f32[32,256]{1,0:T(8,128)S(1)} %get-tuple-element.5, f32[32,2048,256]{2,1,0:T(8,128)} %get-tuple-element.6, pred[256,2048]{0,1:T(8,128)(4,1)S(1)} %fusion.60), kind=kOutput, calls=%fused_computation.46 | convolution fusion | flops 2231894016 | bytes 77135872 | tf_op jit(solution)/shard_map/grqk,kgd->qrgd/dot_general | solution.py:24
  150.9 5.9 %fusion.57 = (f32[256]{0:T(256)S(1)}, bf16[256,2048]{1,0:T(8,128)(2,1)S(1)}) fusion(bf16[256,2048]{1,0:T(8,128)(2,1)S(1)} %copy-done, bf16[256,32,64]{0,2,1:T(8,128)(2,1)S(1)} %fusion.64, bf16[1,32,64,2048]{3,2,1,0:T(8,128)(2,1)} %param.19), kind=kOutput, calls=%fused_computation.40 | convolution fusion | flops 2150104832 | bytes 11535360 | tf_op jit(solution)/shard_map/qrgd,rgdm->qm/dot_general | solution.py:25
  156.8 16.5 %fusion.10 = bf16[256,8192]{1,0:T(8,128)(2,1)} fusion(bf16[1,2048,8192]{2,1,0:T(8,128)(2,1)} %param.21, bf16[256,2048]{1,0:T(8,128)(2,1)S(1)} %get-tuple-element.8, f32[2048]{0:T(1024)S(1)} %bitcast.98, f32[256]{0:T(256)S(1)} %add_rsqrt_fusion), kind=kOutput, calls=%fused_computation.15 | convolution fusion | flops 8594128896 | bytes 38806528 | tf_op jit(solution)/shard_map/dot_general | solution.py:28
  173.3 28.2 %fusion.49 = bf16[256,2048]{1,0:T(8,128)(2,1)} fusion(bf16[256,2048]{1,0:T(8,128)(2,1)S(1)} %get-tuple-element.8, bf16[1,8192,2048]{2,1,0:T(8,128)(2,1)} %param.23, bf16[1,2048,8192]{2,1,0:T(8,128)(2,1)} %param.22, bf16[256,8192]{1,0:T(8,128)(2,1)} %fusion.10, f32[2048]{0:T(1024)S(1)} %bitcast.99, f32[256]{0:T(256)S(1)} %add_rsqrt_fusion), kind=kOutput, calls=%fused_computation.36 | convolution fusion | flops 17203462144 | bytes 73409536 | tf_op jit(solution)/shard_map/dot_general | solution.py:31
  (5 shorter events, 0.0 us)
Async XLA Ops:
  6.5 64.3 %all-gather.6.cloned.1.call-start = ((), (), s32[]{:S(2)}) async-start(), calls=%async_computation.1 | async-start | bytes 9437184 | tf_op jit(solution)/shard_map/all_gather | solution.py:43
  8.8 7.7 %copy-start = (bf16[256,2048]{1,0:T(8,128)(2,1)S(1)}, bf16[256,2048]{1,0:T(8,128)(2,1)}, u32[]{:S(2)}) copy-start(bf16[256,2048]{1,0:T(8,128)(2,1)} %param.12) | copy-start | bytes 3145732
  16.4 106.9 %all-gather.4.cloned.1.call-start = ((), (), s32[]{:S(2)}) async-start(), calls=%async_computation | async-start | bytes 9437184 | tf_op jit(solution)/shard_map/all_gather | solution.py:44
  16.5 7.3 %copy-start.1 = (bf16[1,2048]{1,0:T(2,128)(2,1)S(1)}, bf16[1,2048]{1,0:T(2,128)(2,1)}, u32[]{:S(2)}) copy-start(bf16[1,2048]{1,0:T(2,128)(2,1)} %param.17) | copy-start | bytes 12292
  16.5 7.3 %copy-start.2 = (bf16[1,2048]{1,0:T(2,128)(2,1)S(1)}, bf16[1,2048]{1,0:T(2,128)(2,1)}, u32[]{:S(2)}) copy-start(bf16[1,2048]{1,0:T(2,128)(2,1)} %param.20) | copy-start | bytes 12292
  16.5 7.3 %copy-start.3 = (s32[256]{0:T(256)S(1)}, s32[256]{0:T(256)}, u32[]{:S(2)}) copy-start(s32[256]{0:T(256)} %param.13) | copy-start | bytes 3076
Sparse Core Ops, SparseCore 0:
  16.5 54.3 all-gather.5
  72.5 50.7 all-gather.3
where the time goes:
time: 209 us; the launch traced here: 208 us
  matrix products  125 us (60%)
  waiting for transfers between devices  30.5 us (15%)
  other arithmetic  26.7 us (13%)
  between operations  13.6 us (7%)
  blocking collectives  12.5 us (6%)
    dot_general x1, matrix products, cross_layer(): jnp.dot(act_val, down_w, preferred_element_type=jnp.float32)  28.2 us
    dot_general x1, matrix products, cross_layer(): jnp.einsum('grqk,kgd->qrgd', probs, val_all, preferred_element_type=jnp.f...  27.6 us
    dot_general x1, matrix products, cross_layer(): jnp.einsum('qrgd,kgd->grqk', query, key_all, preferred_element_type=jnp.f...  27.2 us
    all_gather x1, waiting for transfers between devices, body(): key_all = lax.all_gather(key_loc, 'sp', axis=0, tiled=True)  26.8 us
    reduce_sum x1, other arithmetic, cross_layer(): probs = jax.nn.softmax(scores, axis=-1).astype(jnp.bfloat16)  21.6 us
    unnamed x3, matrix products  19.6 us
    dot_general x1, matrix products, cross_layer(): jnp.dot(u_mlp, gate_w, preferred_element_type=jnp.float32)  16.5 us
    all_gather x1, blocking collectives, body(): seg_all = lax.all_gather(seg_ids, 'sp', axis=0, tiled=True)  12.5 us
  transfers between devices with their start and end apart: 2, of which 2 were waited for; matrix products, arithmetic and copies ran while one was open for 31% of the time, Pallas kernels for 0%

commit v1 on v0

v1 whole, which is shorter than its diff:
```python
import functools
import jax
import jax.numpy as jnp
from jax import lax
from jax.experimental import pallas as pl
from jax.experimental.pallas import tpu as pltpu
from jax.sharding import PartitionSpec as P

NORM_EPS = 1e-6
MESH = pl.DeviceIdType.MESH
LOG2E = 1.4426950408889634
BIG = 2.0 ** 127
NT = (((1,), (1,)), ((), ()))
F32 = jnp.float32
BF16 = jnp.bfloat16


def dest_of(me, n, step):
    chips = n // 2
    q = step // 2
    half = chips // 2
    d_chip = jnp.where(q == 0, half, jnp.where(q == 1, 1, jnp.where(q == chips - 1, 0, chips - 1)))
    d_core = jnp.where(q == chips - 1, 1 - lax.rem(step, 2), lax.rem(step, 2))
    chip = lax.rem(me // 2 + d_chip, chips)
    core = lax.rem(lax.rem(me, 2) + d_core, 2)
    return chip * 2 + core


def attn_kernel(n, heads, hd, hid_ref, seg_ref, gkv_ref, gq_ref, wk_hbm, wq_hbm, wv_hbm, o_ref,
                ukv, uq, wbuf, ks, qs, vs, kr, qr, vr, segr, fk, fq, osend, orecv,
                wsem, ssem, rsem, seg_ss, seg_rs, o_ss, o_rs):
    me = lax.axis_index('sp')
    tokens, d_model = hid_ref.shape
    hw = heads * hd
    pw = 2 * hd
    groups = heads // 2

    def wcopy(step, slot):
        d = dest_of(me, n, step)
        rows = pl.ds(pl.multiple_of(d * hw, hw), hw)
        return [pltpu.make_async_copy(w.at[rows, :], wbuf.at[slot, i], wsem.at[slot, i])
                for i, w in enumerate((wk_hbm, wq_hbm, wv_hbm))]

    for slot in range(2):
        for c in wcopy(slot, slot):
            c.start()

    barrier = pltpu.get_barrier_semaphore()
    for off in range(1, n):
        pl.semaphore_signal(barrier, inc=1, device_id={'sp': lax.rem(me + off, n)}, device_id_type=MESH)

    x = hid_ref[...].astype(F32)
    inv = lax.rsqrt(jnp.mean(x * x, axis=-1, keepdims=True) + NORM_EPS)
    xn = x * inv
    ukv[...] = (xn * gkv_ref[...].astype(F32)).astype(BF16)
    uq[...] = (xn * gq_ref[...].astype(F32)).astype(BF16)
    segr[me] = seg_ref[...]

    pl.semaphore_wait(barrier, n - 1)

    def seg_copy(p):
        return pltpu.make_async_remote_copy(seg_ref, segr.at[me], seg_ss.at[p], seg_rs.at[me],
                                            device_id={'sp': p}, device_id_type=MESH)

    def qkv_copies(g, step, p):
        bufs = ((ks, kr), (qs, qr), (vs, vr))
        return [pltpu.make_async_remote_copy(s.at[g, step], r.at[g, me], ssem.at[g, i, step], rsem.at[g, i, me],
                                             device_id={'sp': p}, device_id_type=MESH)
                for i, (s, r) in enumerate(bufs)]

    def project(slot):
        k = lax.dot_general(ukv[...], wbuf[slot, 0], NT, preferred_element_type=F32).astype(BF16)
        q = lax.dot_general(wbuf[slot, 1], uq[...], NT, preferred_element_type=F32).astype(BF16)
        v = lax.dot_general(wbuf[slot, 2], ukv[...], NT, preferred_element_type=F32).astype(BF16)
        return k, q, v

    for off in range(1, n):
        seg_copy(lax.rem(me + off, n)).start()

    def proj_step(step, _):
        slot = lax.rem(step, 2)
        for c in wcopy(step, slot):
            c.wait()
        k, q, v = project(slot)
        for g in range(groups):
            ks[g, step] = k[:, g * pw:(g + 1) * pw]
            qs[g, step] = q[g * pw:(g + 1) * pw]
            vs[g, step] = v[g * pw:(g + 1) * pw]
        for c in qkv_copies(0, step, dest_of(me, n, step)):
            c.start()

        @pl.when(step + 2 < n)
        def _():
            for c in wcopy(step + 2, slot):
                c.start()
        return 0

    lax.fori_loop(0, n - 1, proj_step, 0)
    for g in range(1, groups):
        for step in range(n - 1):
            for c in qkv_copies(g, step, dest_of(me, n, step)):
                c.start()
    for c in wcopy(n - 1, (n - 1) % 2):
        c.wait()
    k, q, v = project((n - 1) % 2)
    for g in range(groups):
        kr[g, me] = k[:, g * pw:(g + 1) * pw]
        qr[g, me] = q[g * pw:(g + 1) * pw]
        vr[g, me] = v[g * pw:(g + 1) * pw]

    for off in range(1, n):
        p = lax.rem(me + off, n)
        pltpu.make_async_remote_copy(seg_ref, segr.at[p], seg_ss.at[p], seg_rs.at[p],
                                     device_id={'sp': p}, device_id_type=MESH).wait_recv()
    ids = lax.broadcasted_iota(jnp.int32, (128, tokens), 0)
    for p in range(n):
        same = ids == segr[p]
        fq[p] = jnp.where(same, 1.0, 0.0).astype(BF16)
        fk[p] = jnp.where(same, 0.0, -BIG).T.astype(BF16)

    scale = (hd ** -0.5) * LOG2E
    kpos = lax.broadcasted_iota(jnp.int32, (tokens, tokens), 0)
    qpos = lax.broadcasted_iota(jnp.int32, (tokens, tokens), 1)
    zero = jnp.zeros((hd, tokens), BF16)

    for g in range(groups):
        for off in range(1, n):
            p = lax.rem(me + off, n)
            for i, r in enumerate((kr, qr, vr)):
                pltpu.make_async_remote_copy(r.at[g, p], r.at[g, p], ssem.at[g, i, 0], rsem.at[g, i, p],
                                             device_id={'sp': p}, device_id_type=MESH).wait_recv()

        def q_step(step, _):
            j = dest_of(me, n, step)
            qa = jnp.concatenate([qr[g, j, 0:hd], zero, fq[j]], axis=0)
            qb = jnp.concatenate([zero, qr[g, j, hd:pw], fq[j]], axis=0)

            def scores(i):
                kx = jnp.concatenate([kr[g, i], fk[i]], axis=1)
                return (jnp.dot(kx, qa, preferred_element_type=F32), jnp.dot(kx, qb, preferred_element_type=F32))

            def first(s, v):
                s = jnp.where(kpos <= qpos, s, -BIG)
                m = jnp.max(s, axis=0, keepdims=True)
                p = jnp.exp2((s - m) * scale)
                l = jnp.sum(p, axis=0, keepdims=True)
                return m, l, jnp.dot(v, p.astype(BF16), preferred_element_type=F32)

            def more(s, v, m, l, acc):
                m2 = jnp.maximum(m, jnp.max(s, axis=0, keepdims=True))
                p = jnp.exp2((s - m2) * scale)
                al = jnp.exp2((m - m2) * scale)
                l = l * al + jnp.sum(p, axis=0, keepdims=True)
                return m2, l, acc * al + jnp.dot(v, p.astype(BF16), preferred_element_type=F32)

            sa, sb = scores(j)
            ca = first(sa, vr[g, j, 0:hd])
            cb = first(sb, vr[g, j, hd:pw])

            def body(i, c):
                sa, sb = scores(i)
                return more(sa, vr[g, i, 0:hd], *c[:3]) + more(sb, vr[g, i, hd:pw], *c[3:])

            ma, la, acca, mb, lb, accb = lax.fori_loop(0, j, body, ca + cb)
            ot = jnp.concatenate([acca / la, accb / lb], axis=0).T.astype(BF16)

            @pl.when(step < n - 1)
            def _():
                osend[g, step] = ot
                pltpu.make_async_remote_copy(
                    osend.at[g, step], orecv.at[:, pl.ds(pl.multiple_of(me * hw + g * pw, pw), pw)],
                    o_ss.at[g, step], o_rs.at[g, me], device_id={'sp': j}, device_id_type=MESH).start()

            @pl.when(step == n - 1)
            def _():
                orecv[:, pl.ds(pl.multiple_of(me * hw + g * pw, pw), pw)] = ot
            return 0

        lax.fori_loop(0, n, q_step, 0)

    for g in range(groups):
        for step in range(n - 1):
            p = dest_of(me, n, step)
            pltpu.make_async_remote_copy(
                osend.at[g, step], orecv.at[:, pl.ds(pl.multiple_of(p * hw + g * pw, pw), pw)],
                o_ss.at[g, step], o_rs.at[g, p], device_id={'sp': p}, device_id_type=MESH).wait_recv()
    o_ref[...] = orecv[...]
    for g in range(groups):
        for step in range(n - 1):
            p = dest_of(me, n, step)
            for c in qkv_copies(g, step, p):
                c.wait_send()
            pltpu.make_async_remote_copy(
                osend.at[g, step], orecv.at[:, pl.ds(pl.multiple_of(me * hw + g * pw, pw), pw)],
                o_ss.at[g, step], o_rs.at[g, me], device_id={'sp': p}, device_id_type=MESH).wait_send()
    for off in range(1, n):
        seg_copy(lax.rem(me + off, n)).wait_send()


def attention(n, hidden, seg_ids, g_kv, g_q, w_key, w_value, w_query):
    tokens, d_model = hidden.shape
    _, q_heads, hd = w_query.shape
    heads = q_heads // n
    hw, pw, groups = heads * hd, 2 * hd, heads // 2
    flat = lambda w: w.transpose(1, 2, 0).reshape(q_heads * hd, d_model)
    vm = pl.BlockSpec(memory_space=pltpu.VMEM)
    hbm = pl.BlockSpec(memory_space=pl.ANY)
    dma = pltpu.SemaphoreType.DMA
    kshape, tshape = (groups, n, tokens, pw), (groups, n, pw, tokens)
    return pl.pallas_call(
        functools.partial(attn_kernel, n, heads, hd),
        out_shape=jax.ShapeDtypeStruct((tokens, n * hw), BF16),
        in_specs=[vm] * 4 + [hbm] * 3,
        out_specs=vm,
        scratch_shapes=[
            pltpu.VMEM((tokens, d_model), BF16), pltpu.VMEM((tokens, d_model), BF16),
            pltpu.VMEM((2, 3, hw, d_model), BF16),
            pltpu.VMEM(kshape, BF16), pltpu.VMEM(tshape, BF16), pltpu.VMEM(tshape, BF16),
            pltpu.VMEM(kshape, BF16), pltpu.VMEM(tshape, BF16), pltpu.VMEM(tshape, BF16),
            pltpu.VMEM((n, 1, tokens), jnp.int32),
            pltpu.VMEM((n, tokens, 128), BF16), pltpu.VMEM((n, 128, tokens), BF16),
            pltpu.VMEM(kshape, BF16), pltpu.VMEM((tokens, n * hw), BF16),
            dma((2, 3)), dma((groups, 3, n)), dma((groups, 3, n)), dma((n,)), dma((n,)), dma((groups, n)), dma((groups, n)),
        ],
        compiler_params=pltpu.CompilerParams(collective_id=0, has_side_effects=True, vmem_limit_bytes=60 * 2 ** 20),
    )(hidden, seg_ids.reshape(1, tokens), g_kv.reshape(1, d_model), g_q.reshape(1, d_model),
      flat(w_key), flat(w_query), flat(w_value))


def mlp_kernel(tile, depth, o_ref, h_ref, gm_ref, wo_hbm, wg_hbm, wu_hbm, wd_hbm, out_ref,
               wo, rg, ru, rd, u, h1, acc, cbuf, so, sg, su, sd):
    tokens, d_model = h_ref.shape
    ff = wg_hbm.shape[1]
    nf = ff // tile
    no = d_model // tile

    def cols(f):
        return pl.ds(pl.multiple_of(f * tile, tile), tile)

    def cg(f):
        s = lax.rem(f, depth)
        return pltpu.make_async_copy(wg_hbm.at[:, cols(f)], rg.at[s], sg.at[s])

    def cu(f):
        s = lax.rem(f, depth)
        return pltpu.make_async_copy(wu_hbm.at[:, cols(f)], ru.at[s], su.at[s])

    def cd(f):
        s = lax.rem(f, depth)
        return pltpu.make_async_copy(wd_hbm.at[cols(f), :], rd.at[s], sd.at[s])

    co = [pltpu.make_async_copy(wo_hbm.at[:, cols(i)], wo.at[i], so.at[i]) for i in range(no)]
    for c in co:
        c.start()
    for f in range(depth):
        cg(jnp.int32(f)).start()
        cu(jnp.int32(f)).start()
        cd(jnp.int32(f)).start()

    ssq = jnp.zeros((tokens, 1), F32)
    for i in range(no):
        co[i].wait()
        a = jnp.dot(o_ref[...], wo[i], preferred_element_type=F32).astype(BF16)
        s = pl.ds(i * tile, tile)
        h = (h_ref[:, s].astype(F32) + a.astype(F32)).astype(BF16)
        h1[:, s] = h
        h = h.astype(F32)
        ssq += jnp.sum(h * h, axis=-1, keepdims=True)
    inv = lax.rsqrt(ssq / d_model + NORM_EPS)
    u[...] = (h1[...].astype(F32) * inv * gm_ref[...].astype(F32)).astype(BF16)

    def gate_up(f):
        s = lax.rem(f, depth)
        cg(f).wait()
        cu(f).wait()
        a = jnp.dot(u[...], rg[s], preferred_element_type=F32).astype(BF16).astype(F32)
        b = jnp.dot(u[...], ru[s], preferred_element_type=F32).astype(BF16).astype(F32)

        @pl.when(f + depth < nf)
        def _():
            cg(f + depth).start()
            cu(f + depth).start()
        return (jax.nn.silu(a) * b).astype(BF16)

    def down(f, c):
        s = lax.rem(f, depth)
        cd(f).wait()
        d = jnp.dot(c, rd[s], preferred_element_type=F32)

        @pl.when(f + depth < nf)
        def _():
            cd(f + depth).start()
        return d

    cbuf[0] = gate_up(jnp.int32(0))
    acc[...] = jnp.zeros_like(acc)

    def step(f, _):
        acc[...] += down(f - 1, cbuf[lax.rem(f - 1, 2)])
        cbuf[lax.rem(f, 2)] = gate_up(f)
        return 0

    lax.fori_loop(1, nf, step, 0)
    d = acc[...] + down(jnp.int32(nf - 1), cbuf[(nf - 1) % 2])
    out_ref[...] = (h1[...].astype(F32) + d.astype(BF16).astype(F32)).astype(BF16)


def mlp(o, hidden, g_mlp, w_out, w_gate, w_up, w_down):
    tokens, d_model = hidden.shape
    ff = w_gate.shape[1]
    tile, depth = 512, 4
    vm = pl.BlockSpec(memory_space=pltpu.VMEM)
    hbm = pl.BlockSpec(memory_space=pl.ANY)
    dma = pltpu.SemaphoreType.DMA
    no = d_model // tile
    return pl.pallas_call(
        functools.partial(mlp_kernel, tile, depth),
        out_shape=jax.ShapeDtypeStruct((tokens, d_model), BF16),
        in_specs=[vm] * 3 + [hbm] * 4,
        out_specs=vm,
        scratch_shapes=[
            pltpu.VMEM((no, d_model, tile), BF16),
            pltpu.VMEM((depth, d_model, tile), BF16), pltpu.VMEM((depth, d_model, tile), BF16),
            pltpu.VMEM((depth, tile, d_model), BF16),
            pltpu.VMEM((tokens, d_model), BF16), pltpu.VMEM((tokens, d_model), BF16),
            pltpu.VMEM((tokens, d_model), F32), pltpu.VMEM((2, tokens, tile), BF16),
            dma((no,)), dma((depth,)), dma((depth,)), dma((depth,)),
        ],
        compiler_params=pltpu.CompilerParams(vmem_limit_bytes=60 * 2 ** 20),
    )(o, hidden, g_mlp.reshape(1, d_model), w_out.reshape(-1, d_model), w_gate, w_up, w_down)


def solution(mesh):
    n = mesh.shape['sp']

    def body(hidden, seg_ids, norm_kv, w_key, w_value, norm_attn, w_query, w_out, norm_mlp, w_gate, w_up, w_down):
        o = attention(n, hidden, seg_ids, norm_kv, norm_attn[0], w_key, w_value, w_query[0])
        return mlp(o, hidden, norm_mlp[0], w_out[0], w_gate[0], w_up[0], w_down[0])

    row_spec = P(('dp', 'sp'), None)
    in_specs = (row_spec, P(('dp', 'sp'))) + (P(),) * 10
    return jax.shard_map(body, mesh=mesh, in_specs=in_specs, out_specs=row_spec, check_vma=False)
```

time: 209 us -> 115 us (0.55)
  matrix products: 125 us -> 0 us
  Pallas kernels: 0 us -> 113 us
  waiting for transfers between devices: 30.5 us -> 0 us
  other arithmetic: 26.7 us -> 0 us
  between operations: 13.6 us -> 0.01 us
  blocking collectives: 12.5 us -> 0 us
    pallas_call x0 -> x2, Pallas kernels: none -> 113 us  [the longest x1 66.4 us: attention(): pl.pallas_call(functools.partial(attn_kernel, n, heads, hd), out_shape=ja...]
    dot_general x5 -> x0, matrix products: 105 us -> none  [the longest x1 28.2 us: cross_layer(): jnp.dot(act_val, down_w, preferred_element_type=jnp.float32)]
    all_gather x2 -> x0, waiting for transfers between devices: 30.4 us -> none  [the longest x1 26.8 us: body(): key_all = lax.all_gather(key_loc, 'sp', axis=0, tiled=True)]
    reduce_sum x2 -> x0, other arithmetic: 23.1 us -> none  [the longest x1 21.6 us: cross_layer(): probs = jax.nn.softmax(scores, axis=-1).astype(jnp.bfloat16)]
    unnamed x3 -> x0, matrix products: 19.6 us -> none
    all_gather x1 -> x0, blocking collectives: 12.5 us -> none  [body(): seg_all = lax.all_gather(seg_ids, 'sp', axis=0, tiled=True)]
    convert_element_type x3 -> x0, other arithmetic: 2.95 us -> none  [the longest x1 1.13 us: body(): jnp.einsum('td,dgk->tgk', u_kv, w_key, preferred_element_type=jnp.float32)]
  transfers between devices with their start and end apart: 2 -> 0, of which waited for: 2 -> 0; matrix products, arithmetic and copies ran while one was open for 31% -> 0% of each run, Pallas kernels for 0% -> 0%
where the time goes in v1:
time: 115 us
  Pallas kernels  113 us (98%)
  local copies, waits for them, and re-layouts  1.29 us (1%)
    pallas_call x1, Pallas kernels, attention(): pl.pallas_call(functools.partial(attn_kernel, n, heads, hd), out_shape=ja...  66.4 us
    pallas_call x1, Pallas kernels, mlp(): pl.pallas_call(functools.partial(mlp_kernel, tile, depth), out_shape=jax....  46.9 us

profile of v1, /device:TPU:81, one launch (start us, length us, event | category | flops | bytes accessed | tf_op | source)
XLA Modules:
  0.0 114.6 jit_solution(14280343928623810978)
XLA Ops:
  0.0 1.3 %reshape.16.gkv_ref = bf16[1,2048]{1,0:T(2,128)(2,1)} reshape(bf16[2048]{0:T(1024)(128)(2,1)} %param.14) | data formatting | bytes 8192 | tf_op jit(solution)/shard_map/reshape | solution.py:226
  1.3 66.4 %shard_map.118.o_ref = bf16[256,2048]{1,0:T(8,128)(2,1)} custom-call(bf16[256,2048]{1,0:T(8,128)(2,1)} %h_ref.1, s32[1,256]{1,0:T(1,128)} %bitcast.23, bf16[1,2048]{1,0:T(2,128)(2,1)} %reshape.16.gkv_ref, bf16[1,2048]{1,0:T(2,128)(2,1)} %gq_ref.1, bf16[2048,2048]{1,0:T(8,128)(2,1)} %bitcast.19, bf16[2048,2048]{1,0:T(8,128)(2,1)} %bitcast.20, ...), custom_call_target="tpu_custom_call" | custom-call | tf_op jit(solution)/shard_map/pallas_call | solution.py:210
  67.7 46.9 %shard_map.119 = bf16[256,2048]{1,0:T(8,128)(2,1)} custom-call(bf16[256,2048]{1,0:T(8,128)(2,1)} %shard_map.118.o_ref, bf16[256,2048]{1,0:T(8,128)(2,1)} %h_ref.1, bf16[1,2048]{1,0:T(2,128)(2,1)} %gm_ref.1, bf16[2048,2048]{1,0:T(8,128)(2,1)} %bitcast.22, bf16[2048,8192]{1,0:T(8,128)(2,1)} %bitcast.16, bf16[2048,8192]{1,0:T(8,128)(2,1)} %bitcast.17, ...), custom_call_target="tpu_custom_call" | custom-call | tf_op jit(solution)/shard_map/pallas_call | solution.py:316

commit v2 on v0

v2 whole, which is shorter than its diff:
```python
import functools
import jax
import jax.numpy as jnp
from jax import lax
from jax.experimental import pallas as pl
from jax.experimental.pallas import tpu as pltpu
from jax.sharding import PartitionSpec as P

NORM_EPS = 1e-6
MESH = pl.DeviceIdType.MESH
LOG2E = 1.4426950408889634
BIG = 2.0 ** 127
NT = (((1,), (1,)), ((), ()))
F32 = jnp.float32
BF16 = jnp.bfloat16


def dest_of(me, n, step):
    chips = n // 2
    q = step // 2
    half = chips // 2
    d_chip = jnp.where(q == 0, half, jnp.where(q == 1, 1, jnp.where(q == chips - 1, 0, chips - 1)))
    d_core = jnp.where(q == chips - 1, 1 - lax.rem(step, 2), lax.rem(step, 2))
    chip = lax.rem(me // 2 + d_chip, chips)
    core = lax.rem(lax.rem(me, 2) + d_core, 2)
    return chip * 2 + core


def kernel(n, heads, hd, tile, nr, hid_ref, seg_ref, gkv_ref, gq_ref, gm_ref, wk_hbm, wq_hbm, wv_hbm,
           wo_hbm, wg_hbm, wu_hbm, wd_hbm, out_ref,
           ukv, uq, ring, ks, qs, vs, kr, qr, vr, segr, fk, fq, osend, orecv, s_scr, p_scr, ab, c_ref,
           wsem, sr, ssem, rsem, seg_ss, seg_rs, o_ss, o_rs):
    me = lax.axis_index('sp')
    tokens, d_model = hid_ref.shape
    ff = wg_hbm.shape[1]
    hw = heads * hd
    pw = 2 * hd
    groups = heads // 2
    nf = ff // tile
    no = d_model // tile

    def remote(s, d, ss, rs, p):
        return pltpu.make_async_remote_copy(s, d, ss, rs, device_id={'sp': p}, device_id_type=MESH)

    kp = d_model // tile
    nc = ff // d_model

    def wpieces(slot, i):
        b = slot * 3 + i
        per = tile // hw
        row = lax.rem(b, per) * kp * hw
        return [ring.at[nr - 5 + b // per, pl.ds(pl.multiple_of(row + k * hw, hw), hw)] for k in range(kp)]

    def wcopy(step):
        slot = lax.rem(step, 3)
        d = dest_of(me, n, step)
        rows = pl.ds(pl.multiple_of(d * hw, hw), hw)
        return [pltpu.make_async_copy(w.at[rows, k * tile:(k + 1) * tile], dst, wsem.at[slot, i, k])
                for i, w in enumerate((wk_hbm, wq_hbm, wv_hbm)) for k, dst in enumerate(wpieces(slot, i))]

    def cols(f):
        return pl.ds(pl.multiple_of(f * tile, tile), tile)

    def chunk(w, c, src):
        s = lax.rem(c, nr)
        return pltpu.make_async_copy(src, ring.at[s], sr.at[s])

    def out_copy(i):
        return chunk(wo_hbm, i, wo_hbm.at[:, cols(i)])

    def gate_copy(f):
        return chunk(wg_hbm, no + 2 * f, wg_hbm.at[:, cols(f)])

    def up_copy(f):
        return chunk(wu_hbm, no + 2 * f + 1, wu_hbm.at[:, cols(f)])

    def down_copy(m):
        rows = pl.ds(pl.multiple_of(lax.rem(m, nc) * d_model, d_model), d_model)
        return chunk(wd_hbm, no + 2 * nf + m, wd_hbm.at[rows, cols(m // nc)])

    def refill_gu(f):
        @pl.when(f < nf)
        def _():
            gate_copy(f).start()
            up_copy(f).start()

        @pl.when(f >= nf)
        def _():
            down_copy(2 * (f - nf)).start()
            down_copy(2 * (f - nf) + 1).start()

    for step in range(2):
        for c in wcopy(jnp.int32(step)):
            c.start()

    barrier = pltpu.get_barrier_semaphore()
    for off in range(1, n):
        pl.semaphore_signal(barrier, inc=1, device_id={'sp': lax.rem(me + off, n)}, device_id_type=MESH)

    def gain(ref):
        return jnp.concatenate([ref[i:i + 1].astype(F32) for i in range(d_model // 128)], axis=1)

    x = hid_ref[...].astype(F32)
    xn = x * lax.rsqrt(jnp.mean(x * x, axis=-1, keepdims=True) + NORM_EPS)
    ukv[...] = (xn * gain(gkv_ref)).astype(BF16)
    uq[...] = (xn * gq_ref[...].astype(F32)).astype(BF16)
    segr[me] = seg_ref[...]

    def seg_copy(p):
        return remote(seg_ref, segr.at[me], seg_ss.at[p], seg_rs.at[me], p)

    def qkv_copies(g, step, p):
        bufs = ((ks, kr), (qs, qr), (vs, vr))
        return [remote(s.at[g, step], r.at[g, me], ssem.at[g, i, step], rsem.at[g, i, me], p)
                for i, (s, r) in enumerate(bufs)]

    def project(step):
        for c in wcopy(step):
            c.wait()

        @pl.when(step + 2 < n)
        def _():
            for c in wcopy(step + 2):
                c.start()
        slot = lax.rem(step, 3)

        u_kv = [ukv[:, i * tile:(i + 1) * tile] for i in range(kp)]
        u_q = [uq[:, i * tile:(i + 1) * tile] for i in range(kp)]
        w = [[p[...] for p in wpieces(slot, i)] for i in range(3)]

        def nt(a, b):
            return sum(lax.dot_general(x, y, NT, preferred_element_type=F32) for x, y in zip(a, b)).astype(BF16)

        k, q, v = nt(u_kv, w[0]), nt(w[1], u_q), nt(w[2], u_kv)
        return k, q, v

    def store(step):
        k, q, v = project(step)
        for g in range(groups):
            ks[g, step] = k[:, g * pw:(g + 1) * pw]
            qs[g, step] = q[g * pw:(g + 1) * pw]
            vs[g, step] = v[g * pw:(g + 1) * pw]

    def send(g, step):
        for c in qkv_copies(g, step, dest_of(me, n, step)):
            c.start()

    def proj_step(step, _):
        store(step)

        @pl.when(step == lead_steps - 1)
        def _():
            pl.semaphore_wait(barrier, n - 1)
            for s in range(lead_steps - 1):
                send(0, s)
            for off in range(1, n):
                seg_copy(lax.rem(me + off, n)).start()

        @pl.when(step >= lead_steps - 1)
        def _():
            send(0, step)
        return 0

    lead_steps = 2
    lax.fori_loop(0, n - 1, proj_step, 0)
    for g in range(1, groups):
        for step in range(n - 1):
            send(g, step)
    lead = nr - 5
    for i in range(no):
        out_copy(i).start()
    for f in range((lead - no + 1) // 2):
        gate_copy(f).start()
        if no + 2 * f + 1 < lead:
            up_copy(f).start()
    k, q, v = project(jnp.int32(n - 1))
    for g in range(groups):
        kr[g, me] = k[:, g * pw:(g + 1) * pw]
        qr[g, me] = q[g * pw:(g + 1) * pw]
        vr[g, me] = v[g * pw:(g + 1) * pw]
    for c in range(lead, nr):
        (up_copy if (c - no) % 2 else gate_copy)((c - no) // 2).start()

    for off in range(1, n):
        p = lax.rem(me + off, n)
        remote(seg_ref, segr.at[p], seg_ss.at[p], seg_rs.at[p], p).wait_recv()
    ids = lax.broadcasted_iota(jnp.int32, (128, tokens), 0)

    def features(p, _):
        same = ids == segr[p]
        fq[p] = jnp.where(same, 1.0, 0.0).astype(BF16)
        fk[p] = jnp.where(same, 0.0, -BIG).T.astype(BF16)
        return 0

    lax.fori_loop(0, n, features, 0)

    scale = (hd ** -0.5) * LOG2E
    kpos = lax.broadcasted_iota(jnp.int32, (tokens, tokens), 0)
    qpos = lax.broadcasted_iota(jnp.int32, (tokens, tokens), 1)
    zero = jnp.zeros((hd, tokens), BF16)
    ones = jnp.ones((16, tokens), BF16)
    half = n // 2
    low = jnp.minimum(me, n - 1 - me)

    def o_cols(d, g):
        return orecv.at[:, pl.ds(pl.multiple_of(d * hw + g * pw, pw), pw)]

    def o_copy(g, j):
        return remote(osend.at[g, j], o_cols(me, g), o_ss.at[g, j], o_rs.at[g, me], j)

    def attend(g, j1):
        j2 = n - 1 - j1

        def q_ext(j):
            return (jnp.concatenate([qr[g, j, 0:hd], zero, fq[j]], axis=0),
                    jnp.concatenate([zero, qr[g, j, hd:pw], fq[j]], axis=0))

        qa, qb = q_ext(j1), q_ext(j2)

        def block(t):
            if t < 2:
                return (j1, j2)[t], t == 0
            first = t - 2 < j1
            return jnp.where(first, j1 + 1 - t, n - t), first

        def scores(t):
            i, first = block(t)
            kx = jnp.concatenate([kr[g, i], fk[i]], axis=1)
            for h in range(2):
                if t < 2:
                    q = (qa, qb)[t][h]
                else:
                    q = qb[h] if t > half else jnp.where(first, qa[h], qb[h])
                s_scr[t % 2, h] = jnp.dot(kx, q, preferred_element_type=F32)

        m_a, m_b, m = [None] * 2, [None] * 2, [None] * 2
        acc_a, acc_b, acc = [None] * 2, [None] * 2, [None] * 2
        alpha = {}

        def soft(t):
            for h in range(2):
                s = s_scr[t % 2, h]
                if t < 2:
                    s = jnp.where(kpos <= qpos, s, -BIG)
                    new = jnp.max(s, axis=0, keepdims=True)
                    (m_a, m_b)[t][h] = new
                else:
                    old = m_a[h] if t == 2 else m[h]
                    if t - 2 < half:
                        old = jnp.where(t - 2 == j1, m_b[h], old)
                    new = jnp.maximum(old, jnp.max(s, axis=0, keepdims=True))
                    alpha[t, h] = jnp.exp2((old - new) * scale)
                    m[h] = new
                p_scr[t % 2, h] = jnp.exp2((s - new) * scale).astype(BF16)

        def mix(t):
            i, _ = block(t)
            for h in range(2):
                vx = jnp.concatenate([vr[g, i, h * hd:(h + 1) * hd], ones], axis=0)
                d = jnp.dot(vx, p_scr[t % 2, h], preferred_element_type=F32)
                if t == 0:
                    acc[h] = d
                elif t == 1:
                    acc_b[h] = d
                else:
                    if t - 2 < half:
                        swap = t - 2 == j1
                        acc_a[h] = acc[h] if t == 2 else jnp.where(swap, acc[h], acc_a[h])
                        acc[h] = jnp.where(swap, acc_b[h], acc[h])
                    acc[h] = acc[h] * alpha[t, h] + d

        scores(0)
        for t in range(n + 2):
            if t < n:
                scores(t + 1)
            if t < n + 1:
                soft(t)
            if t >= 1:
                mix(t - 1)
        return [jnp.concatenate([r[h][0:hd] / r[h][hd:hd + 1] for h in range(2)], axis=0).T.astype(BF16)
                for r in (acc_a, acc)]

    def group(g, _):
        for off in range(1, n):
            p = lax.rem(me + off, n)
            for i, r in enumerate((kr, qr, vr)):
                remote(r.at[g, p], r.at[g, p], ssem.at[g, i, 0], rsem.at[g, i, p], p).wait_recv()

        def unit(t, _):
            j1 = lax.rem(low + 1 + t, half)
            for j, o in zip((j1, n - 1 - j1), attend(g, j1)):
                osend[g, j] = o

                @pl.when(j != me)
                def _():
                    o_copy(g, j).start()
            return 0

        lax.fori_loop(0, half, unit, 0)
        orecv[:, pl.ds(pl.multiple_of(me * hw + g * pw, pw), pw)] = osend[g, me]
        return 0

    lax.fori_loop(0, groups, group, 0)

    for g in range(groups):
        for off in range(1, n):
            p = lax.rem(me + off, n)
            remote(osend.at[g, p], o_cols(p, g), o_ss.at[g, p], o_rs.at[g, p], p).wait_recv()

    h1, u = uq, ukv
    ssq = jnp.zeros((tokens, 1), F32)
    for i in range(no):
        out_copy(i).wait()
        a = jnp.dot(orecv[...], ring[i], preferred_element_type=F32).astype(BF16)
        s = pl.ds(i * tile, tile)
        h = (hid_ref[:, s].astype(F32) + a.astype(F32)).astype(BF16)
        h1[:, s] = h
        h = h.astype(F32)
        ssq += jnp.sum(h * h, axis=-1, keepdims=True)
    for i in range(no // 2):
        refill_gu(jnp.int32((nr - no) // 2 + i))
    inv = lax.rsqrt(ssq / d_model + NORM_EPS)
    u[...] = (h1[...].astype(F32) * inv * gm_ref[...].astype(F32)).astype(BF16)

    def gate_up(f):
        gate_copy(f).wait()
        up_copy(f).wait()
        s = lax.rem(no + 2 * f, nr)
        return [jnp.dot(u[...], ring[s + i], preferred_element_type=F32).astype(BF16) for i in range(2)]

    def act(f):
        a = ab[0].astype(F32)
        c_ref[:, cols(f)] = (jax.nn.silu(a) * ab[1].astype(F32)).astype(BF16)

    ab[0], ab[1] = gate_up(jnp.int32(0))
    refill_gu(jnp.int32(nr // 2))

    def mlp_step(f, _):
        a, b = gate_up(f)
        act(f - 1)
        ab[0] = a
        ab[1] = b

        @pl.when(f + nr // 2 < nf + no * nc // 2)
        def _():
            refill_gu(f + nr // 2)
        return 0

    lax.fori_loop(1, nf, mlp_step, 0)
    act(jnp.int32(nf - 1))

    def down_step(j, _):
        d = None
        for i in range(nc):
            m = j * nc + i
            down_copy(m).wait()
            part = jnp.dot(c_ref[:, i * d_model:(i + 1) * d_model], ring[lax.rem(no + 2 * nf + m, nr)],
                           preferred_element_type=F32)
            d = part if d is None else d + part
        out_ref[:, cols(j)] = (h1[:, cols(j)].astype(F32) + d.astype(BF16).astype(F32)).astype(BF16)
        return 0

    lax.fori_loop(0, no, down_step, 0)

    for g in range(groups):
        for step in range(n - 1):
            for c in qkv_copies(g, step, dest_of(me, n, step)):
                c.wait_send()
        for off in range(1, n):
            o_copy(g, lax.rem(me + off, n)).wait_send()
    for off in range(1, n):
        seg_copy(lax.rem(me + off, n)).wait_send()


def decoder(n, hidden, seg_ids, g_kv, g_q, g_mlp, w_key, w_value, w_query, w_out, w_gate, w_up, w_down):
    tokens, d_model = hidden.shape
    _, q_heads, hd = w_query.shape
    heads = q_heads // n
    hw, pw, groups = heads * hd, 2 * hd, heads // 2
    tile, nr = 512, 18
    flat = lambda w: w.transpose(1, 2, 0).reshape(q_heads * hd, d_model)
    row = lambda g: g.reshape(1, d_model)
    vm = pl.BlockSpec(memory_space=pltpu.VMEM)
    hbm = pl.BlockSpec(memory_space=pl.ANY)
    dma = pltpu.SemaphoreType.DMA
    vb = lambda *s: pltpu.VMEM(s, BF16)
    kshape, tshape = (groups, n, tokens, pw), (groups, n, pw, tokens)
    return pl.pallas_call(
        functools.partial(kernel, n, heads, hd, tile, nr),
        out_shape=jax.ShapeDtypeStruct((tokens, d_model), BF16),
        in_specs=[vm] * 5 + [hbm] * 7,
        out_specs=vm,
        scratch_shapes=[
            vb(tokens, d_model), vb(tokens, d_model), vb(nr, d_model, tile),
            vb(*kshape), vb(*tshape), vb(*tshape), vb(*kshape), vb(*tshape), vb(*tshape),
            pltpu.VMEM((n, 1, tokens), jnp.int32), vb(n, tokens, 128), vb(n, 128, tokens),
            vb(*kshape), vb(tokens, n * hw),
            pltpu.VMEM((2, 2, tokens, tokens), F32), vb(2, 2, tokens, tokens),
            vb(2, tokens, tile), vb(tokens, w_gate.shape[1]),
            dma((3, 3, d_model // tile)), dma((nr,)), dma((groups, 3, n)), dma((groups, 3, n)), dma((n,)), dma((n,)),
            dma((groups, n)), dma((groups, n)),
        ],
        compiler_params=pltpu.CompilerParams(collective_id=0, has_side_effects=True, vmem_limit_bytes=67043328),
    )(hidden, seg_ids.reshape(1, tokens), g_kv.reshape(d_model // 128, 128), row(g_q), row(g_mlp), flat(w_key), flat(w_query), flat(w_value),
      w_out.reshape(-1, d_model), w_gate, w_up, w_down)


def solution(mesh):
    n = mesh.shape['sp']

    def body(hidden, seg_ids, norm_kv, w_key, w_value, norm_attn, w_query, w_out, norm_mlp, w_gate, w_up, w_down):
        return decoder(n, hidden, seg_ids, norm_kv, norm_attn[0], norm_mlp[0], w_key, w_value, w_query[0], w_out[0],
                       w_gate[0], w_up[0], w_down[0])

    row_spec = P(('dp', 'sp'), None)
    in_specs = (row_spec, P(('dp', 'sp'))) + (P(),) * 10
    return jax.shard_map(body, mesh=mesh, in_specs=in_specs, out_specs=row_spec, check_vma=False)
```

time: 209 us -> 95.9 us (0.46)
  matrix products: 125 us -> 0 us
  Pallas kernels: 0 us -> 93.5 us
  waiting for transfers between devices: 30.5 us -> 0 us
  other arithmetic: 26.7 us -> 0 us
  between operations: 13.6 us -> 0.01 us
  blocking collectives: 12.5 us -> 0 us
  local copies, waits for them, and re-layouts: 0.02 us -> 2.3 us
    dot_general x5 -> x0, matrix products: 105 us -> none  [the longest x1 28.2 us: cross_layer(): jnp.dot(act_val, down_w, preferred_element_type=jnp.float32)]
    pallas_call x0 -> x1, Pallas kernels: none -> 93.5 us  [decoder(): pl.pallas_call(functools.partial(kernel, n, heads, hd, tile, nr), out_sha...]
    all_gather x2 -> x0, waiting for transfers between devices: 30.4 us -> none  [the longest x1 26.8 us: body(): key_all = lax.all_gather(key_loc, 'sp', axis=0, tiled=True)]
    reduce_sum x2 -> x0, other arithmetic: 23.1 us -> none  [the longest x1 21.6 us: cross_layer(): probs = jax.nn.softmax(scores, axis=-1).astype(jnp.bfloat16)]
    unnamed x3 -> x0, matrix products: 19.6 us -> none
    all_gather x1 -> x0, blocking collectives: 12.5 us -> none  [body(): seg_all = lax.all_gather(seg_ids, 'sp', axis=0, tiled=True)]
    convert_element_type x3 -> x0, other arithmetic: 2.95 us -> none  [the longest x1 1.13 us: body(): jnp.einsum('td,dgk->tgk', u_kv, w_key, preferred_element_type=jnp.float32)]
    unnamed x8 -> x1, local copies, waits for them, and re-layouts: 0.02 us -> 2.3 us
  transfers between devices with their start and end apart: 2 -> 0, of which waited for: 2 -> 0; matrix products, arithmetic and copies ran while one was open for 31% -> 0% of each run, Pallas kernels for 0% -> 0%
where the time goes in v2:
time: 95.9 us; the launch traced here: 95.8 us
  Pallas kernels  93.5 us (97%)
  local copies, waits for them, and re-layouts  2.3 us (2%)
    pallas_call x1, Pallas kernels, decoder(): pl.pallas_call(functools.partial(kernel, n, heads, hd, tile, nr), out_sha...  93.5 us
    unnamed x1, local copies, waits for them, and re-layouts  2.3 us

profile of v2, /device:TPU:81, one launch (start us, length us, event | category | flops | bytes accessed | tf_op | source)
XLA Modules:
  0.0 95.8 jit_solution(5211237492138571788)
XLA Ops:
  0.0 93.5 %shard_map.118 = bf16[256,2048]{1,0:T(8,128)(2,1)} custom-call(bf16[256,2048]{1,0:T(8,128)(2,1)} %hid_ref.1, s32[1,256]{1,0:T(1,128)} %bitcast.25, bf16[16,128]{1,0:T(8,128)(2,1)} %bitcast.24, bf16[1,2048]{1,0:T(2,128)(2,1)} %gq_ref.1, bf16[1,2048]{1,0:T(2,128)(2,1)} %gm_ref.1, bf16[2048,2048]{1,0:T(8,128)(2,1)} %bitcast.20, bf16[2048,2048]{1,0:T(8,128)(2,1)} %bitcast.21, ...), custom_call_target="tpu_custom_call" | custom-call | tf_op jit(solution)/shard_map/pallas_call | solution.py:388
  93.5 2.3 %copy.14 = bf16[256,2048]{1,0:T(8,128)(2,1)} copy(bf16[256,2048]{1,0:T(8,128)(2,1)} %shard_map.118) | data formatting | bytes 2097152

commit v3 on v2

--- a/solution.py
+++ b/solution.py
@@ -15,21 +15,26 @@
 BF16 = jnp.bfloat16
 
 
+def route(me, n):
+    chips = n // 2
+    assert chips == 4
+    chip, core = me // 2, lax.rem(me, 2)
+    turn = 1 - 2 * core
+    ahead = lax.rem(chip + turn + chips, chips) * 2
+    behind = lax.rem(chip - turn + chips, chips) * 2
+    return ahead, behind, chip * 2 + 1 - core, behind + core
+
+
 def dest_of(me, n, step):
-    chips = n // 2
-    q = step // 2
-    half = chips // 2
-    d_chip = jnp.where(q == 0, half, jnp.where(q == 1, 1, jnp.where(q == chips - 1, 0, chips - 1)))
-    d_core = jnp.where(q == chips - 1, 1 - lax.rem(step, 2), lax.rem(step, 2))
-    chip = lax.rem(me // 2 + d_chip, chips)
-    core = lax.rem(lax.rem(me, 2) + d_core, 2)
-    return chip * 2 + core
+    ahead, behind, other, _ = route(me, n)
+    pair = jnp.where(step < 4, behind, ahead) + lax.rem(step, 4)
+    return jnp.where(lax.rem(step, 4) < 2, pair, jnp.where(lax.rem(step, 4) == 2, other, me))
 
 
 def kernel(n, heads, hd, tile, nr, hid_ref, seg_ref, gkv_ref, gq_ref, gm_ref, wk_hbm, wq_hbm, wv_hbm,
            wo_hbm, wg_hbm, wu_hbm, wd_hbm, out_ref,
            ukv, uq, ring, ks, qs, vs, kr, qr, vr, segr, fk, fq, osend, orecv, s_scr, p_scr, ab, c_ref,
-           wsem, sr, ssem, rsem, seg_ss, seg_rs, o_ss, o_rs):
+           wsem, sr, hand_ss, hand_rs, ssem, rsem, seg_ss, seg_rs, o_ss, o_rs):
     me = lax.axis_index('sp')
     tokens, d_model = hid_ref.shape
     ff = wg_hbm.shape[1]
@@ -101,20 +106,31 @@
         return jnp.concatenate([ref[i:i + 1].astype(F32) for i in range(d_model // 128)], axis=1)
 
     x = hid_ref[...].astype(F32)
-    xn = x * lax.rsqrt(jnp.mean(x * x, axis=-1, keepdims=True) + NORM_EPS)
-    ukv[...] = (xn * gain(gkv_ref)).astype(BF16)
-    uq[...] = (xn * gq_ref[...].astype(F32)).astype(BF16)
+
+    def normed(x):
+        xn = x * lax.rsqrt(jnp.mean(x * x, axis=-1, keepdims=True) + NORM_EPS)
+        return (xn * gain(gkv_ref)).astype(BF16), (xn * gq_ref[...].astype(F32)).astype(BF16)
+
+    ukv[...], uq[...] = normed(x)
     segr[me] = seg_ref[...]
 
     def seg_copy(p):
         return remote(seg_ref, segr.at[me], seg_ss.at[p], seg_rs.at[me], p)
 
-    def qkv_copies(g, step, p):
+    ahead, _, _, origin = route(me, n)
+    handed = c_ref.at[:, 0:d_model]
+    y_kv = c_ref.at[:, d_model:2 * d_model]
+    y_q = c_ref.at[:, 2 * d_model:3 * d_model]
+    hand = remote(hid_ref, handed, hand_ss, hand_rs, ahead + lax.rem(me, 2))
+
+    def qkv_copies(g, step):
+        slot = step - step // 4
+        shard = jnp.where(step < 4, me, origin)
         bufs = ((ks, kr), (qs, qr), (vs, vr))
-        return [remote(s.at[g, step], r.at[g, me], ssem.at[g, i, step], rsem.at[g, i, me], p)
+        return [remote(s.at[g, slot], r.at[g, shard], ssem.at[g, i, slot], rsem.at[g, i, shard], dest_of(me, n, step))
                 for i, (s, r) in enumerate(bufs)]
 
-    def project(step):
+    def project(step, xkv, xq):
         for c in wcopy(step):
             c.wait()
 
@@ -124,8 +140,8 @@
                 c.start()
         slot = lax.rem(step, 3)
 
-        u_kv = [ukv[:, i * tile:(i + 1) * tile] for i in range(kp)]
-        u_q = [uq[:, i * tile:(i + 1) * tile] for i in range(kp)]
+        u_kv = [xkv[:, i * tile:(i + 1) * tile] for i in range(kp)]
+        u_q = [xq[:, i * tile:(i + 1) * tile] for i in range(kp)]
         w = [[p[...] for p in wpieces(slot, i)] for i in range(3)]
 
         def nt(a, b):
@@ -134,38 +150,40 @@
         k, q, v = nt(u_kv, w[0]), nt(w[1], u_q), nt(w[2], u_kv)
         return k, q, v
 
-    def store(step):
-        k, q, v = project(step)
+    def store(step, xkv, xq):
+        slot = step - step // 4
+        k, q, v = project(step, xkv, xq)
         for g in range(groups):
-            ks[g, step] = k[:, g * pw:(g + 1) * pw]
-            qs[g, step] = q[g * pw:(g + 1) * pw]
-            vs[g, step] = v[g * pw:(g + 1) * pw]
+            ks[g, slot] = k[:, g * pw:(g + 1) * pw]
+            qs[g, slot] = q[g * pw:(g + 1) * pw]
+            vs[g, slot] = v[g * pw:(g + 1) * pw]
+
+    def keep(step, shard, xkv, xq):
+        k, q, v = project(step, xkv, xq)
+        for g in range(groups):
+            kr[g, shard] = k[:, g * pw:(g + 1) * pw]
+            qr[g, shard] = q[g * pw:(g + 1) * pw]
+            vr[g, shard] = v[g * pw:(g + 1) * pw]
 
     def send(g, step):
-        for c in qkv_copies(g, step, dest_of(me, n, step)):
+        for c in qkv_copies(g, step):
             c.start()
 
-    def proj_step(step, _):
-        store(step)
-
-        @pl.when(step == lead_steps - 1)
+    def own_step(step, _):
+        store(step, ukv, uq)
+
+        @pl.when(step == 1)
         def _():
             pl.semaphore_wait(barrier, n - 1)
-            for s in range(lead_steps - 1):
-                send(0, s)
+            hand.start()
             for off in range(1, n):
                 seg_copy(lax.rem(me + off, n)).start()
-
-        @pl.when(step >= lead_steps - 1)
-        def _():
-            send(0, step)
-        return 0
-
-    lead_steps = 2
-    lax.fori_loop(0, n - 1, proj_step, 0)
-    for g in range(1, groups):
-        for step in range(n - 1):
-            send(g, step)
+        return 0
+
+    lax.fori_loop(0, 3, own_step, 0)
+    for g in range(groups):
+        send(g, 2)
+    keep(jnp.int32(3), me, ukv, uq)
     lead = nr - 5
     for i in range(no):
         out_copy(i).start()
@@ -173,11 +191,26 @@
         gate_copy(f).start()
         if no + 2 * f + 1 < lead:
             up_copy(f).start()
-    k, q, v = project(jnp.int32(n - 1))
+    hand.wait_send()
     for g in range(groups):
-        kr[g, me] = k[:, g * pw:(g + 1) * pw]
-        qr[g, me] = q[g * pw:(g + 1) * pw]
-        vr[g, me] = v[g * pw:(g + 1) * pw]
+        for step in range(2):
+            send(g, step)
+    hand.wait_recv()
+    y_kv[...], y_q[...] = normed(handed[...].astype(F32))
+
+    def handed_step(step, _):
+        store(step, y_kv, y_q)
+        send(0, step)
+        return 0
+
+    lax.fori_loop(4, 6, handed_step, 0)
+    for g in range(1, groups):
+        for step in (4, 5):
+            send(g, step)
+    lax.fori_loop(6, 7, handed_step, 0)
+    for g in range(1, groups):
+        send(g, 6)
+    keep(jnp.int32(7), origin, y_kv, y_q)
     for c in range(lead, nr):
         (up_copy if (c - no) % 2 else gate_copy)((c - no) // 2).start()
 
@@ -283,8 +316,11 @@
     def group(g, _):
         for off in range(1, n):
             p = lax.rem(me + off, n)
-            for i, r in enumerate((kr, qr, vr)):
-                remote(r.at[g, p], r.at[g, p], ssem.at[g, i, 0], rsem.at[g, i, p], p).wait_recv()
+
+            @pl.when(p != origin)
+            def _():
+                for i, r in enumerate((kr, qr, vr)):
+                    remote(r.at[g, p], r.at[g, p], ssem.at[g, i, 0], rsem.at[g, i, p], p).wait_recv()
 
         def unit(t, _):
             j1 = lax.rem(low + 1 + t, half)
@@ -363,8 +399,8 @@
     lax.fori_loop(0, no, down_step, 0)
 
     for g in range(groups):
-        for step in range(n - 1):
-            for c in qkv_copies(g, step, dest_of(me, n, step)):
+        for step in (0, 1, 2, 4, 5, 6):
+            for c in qkv_copies(g, step):
                 c.wait_send()
         for off in range(1, n):
             o_copy(g, lax.rem(me + off, n)).wait_send()
@@ -392,12 +428,12 @@
         out_specs=vm,
         scratch_shapes=[
             vb(tokens, d_model), vb(tokens, d_model), vb(nr, d_model, tile),
-            vb(*kshape), vb(*tshape), vb(*tshape), vb(*kshape), vb(*tshape), vb(*tshape),
+            vb(groups, 6, tokens, pw), vb(groups, 6, pw, tokens), vb(groups, 6, pw, tokens), vb(*kshape), vb(*tshape), vb(*tshape),
             pltpu.VMEM((n, 1, tokens), jnp.int32), vb(n, tokens, 128), vb(n, 128, tokens),
             vb(*kshape), vb(tokens, n * hw),
             pltpu.VMEM((2, 2, tokens, tokens), F32), vb(2, 2, tokens, tokens),
             vb(2, tokens, tile), vb(tokens, w_gate.shape[1]),
-            dma((3, 3, d_model // tile)), dma((nr,)), dma((groups, 3, n)), dma((groups, 3, n)), dma((n,)), dma((n,)),
+            dma((3, 3, d_model // tile)), dma((nr,)), dma, dma, dma((groups, 3, 6)), dma((groups, 3, n)), dma((n,)), dma((n,)),
             dma((groups, n)), dma((groups, n)),
         ],
         compiler_params=pltpu.CompilerParams(collective_id=0, has_side_effects=True, vmem_limit_bytes=67043328),

time: 95.9 us -> 90.8 us (0.947); the launches traced: 95.8 us -> 89.5 us
  Pallas kernels: 93.5 us -> 87.2 us
    pallas_call x1, Pallas kernels: 93.5 us -> 87.2 us  [decoder(): pl.pallas_call(functools.partial(kernel, n, heads, hd, tile, nr), out_sha...]
where the time goes in v3:
time: 90.8 us; the launch traced here: 89.5 us
  Pallas kernels  87.2 us (96%)
  local copies, waits for them, and re-layouts  2.3 us (3%)
    pallas_call x1, Pallas kernels, decoder(): pl.pallas_call(functools.partial(kernel, n, heads, hd, tile, nr), out_sha...  87.2 us
    unnamed x1, local copies, waits for them, and re-layouts  2.3 us

profile of v3, /device:TPU:81, one launch (start us, length us, event | category | flops | bytes accessed | tf_op | source)
XLA Modules:
  0.0 89.5 jit_solution(4653890514704794560)
XLA Ops:
  0.0 87.2 %shard_map.118 = bf16[256,2048]{1,0:T(8,128)(2,1)} custom-call(bf16[256,2048]{1,0:T(8,128)(2,1)} %hid_ref.1, s32[1,256]{1,0:T(1,128)} %bitcast.25, bf16[16,128]{1,0:T(8,128)(2,1)} %bitcast.24, bf16[1,2048]{1,0:T(2,128)(2,1)} %gq_ref.1, bf16[1,2048]{1,0:T(2,128)(2,1)} %gm_ref.1, bf16[2048,2048]{1,0:T(8,128)(2,1)} %bitcast.20, bf16[2048,2048]{1,0:T(8,128)(2,1)} %bitcast.21, ...), custom_call_target="tpu_custom_call" | custom-call | tf_op jit(solution)/shard_map/pallas_call | solution.py:424
  87.2 2.3 %copy.14 = bf16[256,2048]{1,0:T(8,128)(2,1)} copy(bf16[256,2048]{1,0:T(8,128)(2,1)} %shard_map.118) | data formatting | bytes 2097152

commit v4 on v3

--- a/solution.py
+++ b/solution.py
@@ -172,7 +172,7 @@
     def own_step(step, _):
         store(step, ukv, uq)
 
-        @pl.when(step == 1)
+        @pl.when(step == 0)
         def _():
             pl.semaphore_wait(barrier, n - 1)
             hand.start()
@@ -192,9 +192,8 @@
         if no + 2 * f + 1 < lead:
             up_copy(f).start()
     hand.wait_send()
-    for g in range(groups):
-        for step in range(2):
-            send(g, step)
+    for step in range(2):
+        send(0, step)
     hand.wait_recv()
     y_kv[...], y_q[...] = normed(handed[...].astype(F32))
 
@@ -204,6 +203,8 @@
         return 0
 
     lax.fori_loop(4, 6, handed_step, 0)
+    for step in range(2):
+        send(1, step)
     for g in range(1, groups):
         for step in (4, 5):
             send(g, step)
@@ -347,6 +348,7 @@
     ssq = jnp.zeros((tokens, 1), F32)
     for i in range(no):
         out_copy(i).wait()
+    for i in range(no):
         a = jnp.dot(orecv[...], ring[i], preferred_element_type=F32).astype(BF16)
         s = pl.ds(i * tile, tile)
         h = (hid_ref[:, s].astype(F32) + a.astype(F32)).astype(BF16)
@@ -359,37 +361,48 @@
     u[...] = (h1[...].astype(F32) * inv * gm_ref[...].astype(F32)).astype(BF16)
 
     def gate_up(f):
-        gate_copy(f).wait()
-        up_copy(f).wait()
-        s = lax.rem(no + 2 * f, nr)
-        return [jnp.dot(u[...], ring[s + i], preferred_element_type=F32).astype(BF16) for i in range(2)]
+        for i in range(2):
+            gate_copy(f + i).wait()
+            up_copy(f + i).wait()
+        out = []
+        for i in range(2):
+            s = lax.rem(no + 2 * (f + i), nr)
+            out += [jnp.dot(u[...], ring[s + k], preferred_element_type=F32).astype(BF16) for k in range(2)]
+        return out
 
     def act(f):
-        a = ab[0].astype(F32)
-        c_ref[:, cols(f)] = (jax.nn.silu(a) * ab[1].astype(F32)).astype(BF16)
-
-    ab[0], ab[1] = gate_up(jnp.int32(0))
-    refill_gu(jnp.int32(nr // 2))
-
-    def mlp_step(f, _):
-        a, b = gate_up(f)
-        act(f - 1)
-        ab[0] = a
-        ab[1] = b
-
-        @pl.when(f + nr // 2 < nf + no * nc // 2)
-        def _():
-            refill_gu(f + nr // 2)
-        return 0
-
-    lax.fori_loop(1, nf, mlp_step, 0)
-    act(jnp.int32(nf - 1))
+        for i in range(2):
+            a = ab[2 * i].astype(F32)
+            c_ref[:, cols(f + i)] = (jax.nn.silu(a) * ab[2 * i + 1].astype(F32)).astype(BF16)
+
+    def keep_ab(v):
+        for i in range(4):
+            ab[i] = v[i]
+
+    keep_ab(gate_up(jnp.int32(0)))
+    for i in range(2):
+        refill_gu(jnp.int32(nr // 2 + i))
+
+    def mlp_step(t, _):
+        f = 2 * t
+        v = gate_up(f)
+        act(f - 2)
+        keep_ab(v)
+        for i in range(2):
+            @pl.when(f + i + nr // 2 < nf + no * nc // 2)
+            def _():
+                refill_gu(f + i + nr // 2)
+        return 0
+
+    lax.fori_loop(1, nf // 2, mlp_step, 0)
+    act(jnp.int32(nf - 2))
 
     def down_step(j, _):
         d = None
         for i in range(nc):
+            down_copy(j * nc + i).wait()
+        for i in range(nc):
             m = j * nc + i
-            down_copy(m).wait()
             part = jnp.dot(c_ref[:, i * d_model:(i + 1) * d_model], ring[lax.rem(no + 2 * nf + m, nr)],
                            preferred_element_type=F32)
             d = part if d is None else d + part
@@ -432,7 +445,7 @@
             pltpu.VMEM((n, 1, tokens), jnp.int32), vb(n, tokens, 128), vb(n, 128, tokens),
             vb(*kshape), vb(tokens, n * hw),
             pltpu.VMEM((2, 2, tokens, tokens), F32), vb(2, 2, tokens, tokens),
-            vb(2, tokens, tile), vb(tokens, w_gate.shape[1]),
+            vb(4, tokens, tile), vb(tokens, w_gate.shape[1]),
             dma((3, 3, d_model // tile)), dma((nr,)), dma, dma, dma((groups, 3, 6)), dma((groups, 3, n)), dma((n,)), dma((n,)),
             dma((groups, n)), dma((groups, n)),
         ],

time: 90.8 us -> 86.4 us (0.952)
  Pallas kernels: 87.2 us -> 83.5 us
    pallas_call x1, Pallas kernels: 87.2 us -> 83.5 us  [decoder(): pl.pallas_call(functools.partial(kernel, n, heads, hd, tile, nr), out_sha...]
where the time goes in v4:
time: 86.4 us; the launch traced here: 85.9 us
  Pallas kernels  83.5 us (97%)
  local copies, waits for them, and re-layouts  2.3 us (3%)
    pallas_call x1, Pallas kernels, decoder(): pl.pallas_call(functools.partial(kernel, n, heads, hd, tile, nr), out_sha...  83.5 us
    unnamed x1, local copies, waits for them, and re-layouts  2.3 us

profile of v4, /device:TPU:81, one launch (start us, length us, event | category | flops | bytes accessed | tf_op | source)
XLA Modules:
  0.0 85.9 jit_solution(17302272435814634045)
XLA Ops:
  0.0 83.5 %shard_map.118 = bf16[256,2048]{1,0:T(8,128)(2,1)} custom-call(bf16[256,2048]{1,0:T(8,128)(2,1)} %hid_ref.1, s32[1,256]{1,0:T(1,128)} %bitcast.25, bf16[16,128]{1,0:T(8,128)(2,1)} %bitcast.24, bf16[1,2048]{1,0:T(2,128)(2,1)} %gq_ref.1, bf16[1,2048]{1,0:T(2,128)(2,1)} %gm_ref.1, bf16[2048,2048]{1,0:T(8,128)(2,1)} %bitcast.20, bf16[2048,2048]{1,0:T(8,128)(2,1)} %bitcast.21, ...), custom_call_target="tpu_custom_call" | custom-call | tf_op jit(solution)/shard_map/pallas_call | solution.py:437
  83.6 2.3 %copy.14 = bf16[256,2048]{1,0:T(8,128)(2,1)} copy(bf16[256,2048]{1,0:T(8,128)(2,1)} %shard_map.118) | data formatting | bytes 2097152
